TPU v7x, 32 devices: a whole 2x2x4 slice. The times are simulated.
32 devices in a mesh: gx: 2 (over x), gy: 4 (over z), gz: 4 (over y, core).
Axes of the slice: x: 2, y: 2, z: 4, core: 2. Of those that a mesh axis runs over, the one named last changes fastest.
Arguments:
- offsets: float32 [3, 4, 16, 4, 256], P(None, 'gx', 'gy', 'gz'), may hold values from 0 to 1
- velocity: float32 [3, 4, 16, 4, 256], P(None, 'gx', 'gy', 'gz'), may hold values from -6 to 6
- mass: float32 [4, 16, 4, 256], P('gx', 'gy', 'gz'), may hold values from 0.004 to 0.04
- counts: int32 [4, 16, 4], P('gx', 'gy', 'gz'), may hold values from 64 to 256
Outputs:
- new_offsets: float32 [3, 4, 16, 4, 256], P(None, 'gx', 'gy', 'gz')
- new_velocity: float32 [3, 4, 16, 4, 256], P(None, 'gx', 'gy', 'gz')
Inputs may be any that keep to these rules, and one draw needn't show every extreme that they name: `counts`: slots at or past a leaf's count are padding; their masses and positions carry no meaning as sources.
All inputs are finite; a program needn't handle non-finite values.
Results may differ from a plain program's by a relative error of at most 0.0001.
Values sent between devices are 32-bit elements; how exact they have to be, the bound alone decides.
A program may use at most 64 MiB of HBM per device.

v0:
```python
import jax
import jax.numpy as jnp
import numpy as np
from jax import lax
from jax.sharding import PartitionSpec as P

SUBSTEPS = 2


def with_halo(block, sides, width):
    for axis, dim in sides:
        count = lax.axis_size(axis)
        forward = [(i, i + 1) for i in range(count - 1)]
        forward.append((count - 1, 0))
        backward = [(target, source) for source, target in forward]
        low = lax.ppermute(
            lax.slice_in_dim(block, block.shape[dim] - width, None, axis=dim), axis, forward
        )
        high = lax.ppermute(lax.slice_in_dim(block, 0, width, axis=dim), axis, backward)
        block = jnp.concatenate([low, block, high], axis=dim)
    return block


def pair_tile(target, source_pos, source_mass, shift):
    dist = source_pos[..., None, :] - target[..., :, None]
    dist = dist + shift.reshape((3,) + (1,) * (dist.ndim - 1))
    square = jnp.sum(dist * dist, axis=0)
    factor = (square + 0.01) ** (-1.5) * jnp.maximum(1.0 - square, 0.0) ** 2
    scaled = source_mass[..., None, :] * factor
    return jnp.sum(scaled[None] * dist, axis=-1)


def ghosts(fields):
    return with_halo(fields, (("gx", 1), ("gy", 2), ("gz", 3)), 1)


def forces(position, padded_pos, padded_mass):
    span_x, span_y, span_z, slots = (
        position.shape[1],
        position.shape[2],
        position.shape[3],
        position.shape[4],
    )
    leaves = span_x * span_y * span_z
    block = 4
    blocks = leaves // block
    pos_list = []
    mass_list = []
    shift_list = []
    for step_a in (-1, 0, 1):
        for step_b in (-1, 0, 1):
            for step_c in (-1, 0, 1):
                lower = (1 + step_a, 1 + step_b, 1 + step_c)
                source_pos = padded_pos[
                    :,
                    lower[0] : lower[0] + span_x,
                    lower[1] : lower[1] + span_y,
                    lower[2] : lower[2] + span_z,
                    :,
                ]
                source_mass = padded_mass[
                    lower[0] : lower[0] + span_x,
                    lower[1] : lower[1] + span_y,
                    lower[2] : lower[2] + span_z,
                    :,
                ]
                pos_list.append(source_pos.reshape(3, blocks, block, slots))
                mass_list.append(source_mass.reshape(blocks, block, slots))
                shift_list.append([step_a, step_b, step_c])
    all_pos = jnp.moveaxis(jnp.stack(pos_list), 2, 0)
    all_mass = jnp.moveaxis(jnp.stack(mass_list), 1, 0)
    shifts = jnp.array(np.array(shift_list, dtype=np.float32))
    targets = jnp.moveaxis(position.reshape(3, blocks, block, slots), 1, 0)

    def one_block(items):
        target, source_pos, source_mass = items

        def one_offset(total, parts):
            return (total + pair_tile(target, parts[0], parts[1], parts[2]), None)

        total, _ = lax.scan(one_offset, jnp.zeros_like(target), (source_pos, source_mass, shifts))
        return total

    result = lax.map(one_block, (targets, all_pos, all_mass))
    return jnp.moveaxis(result, 0, 1).reshape(position.shape)


def shards(offsets, velocity, mass, counts):
    slot = jnp.arange(mass.shape[-1], dtype=jnp.int32)
    weight = jnp.where(slot < counts[..., None], mass, jnp.float32(0.0))
    position, speed = (offsets, velocity)
    padded = ghosts(jnp.concatenate([position, weight[None]], axis=0))
    ghost_mass = padded[3]
    padded_pos = padded[:3]
    for step in range(SUBSTEPS):
        if step > 0:
            padded_pos = ghosts(position)
        speed = speed + 0.1 * forces(position, padded_pos, ghost_mass)
        position = position + 0.1 * speed
    return (position, speed)


def solution(mesh):
    return jax.shard_map(
        shards,
        mesh=mesh,
        in_specs=(
            P(None, "gx", "gy", "gz", None),
            P(None, "gx", "gy", "gz", None),
            P("gx", "gy", "gz", None),
            P("gx", "gy", "gz"),
        ),
        out_specs=(P(None, "gx", "gy", "gz", None), P(None, "gx", "gy", "gz", None)),
        check_vma=False,
    )
```

profile of v0, /device:TPU:0, one launch (start us, length us, event | category | flops | bytes accessed | tf_op | source)
XLA Modules:
  0.0 335.7 jit_solution(17466437141599296494)
XLA Ops:
  2.2 3.0 collective-permute-start
  5.3 1.6 collective-permute-done
  6.9 2.0 collective-permute-done.1
  9.0 1.6 collective-permute-start.2
  10.6 2.2 collective-permute-start.3
  12.8 1.7 collective-permute-done.2
  14.7 1.7 collective-permute-start.5
  17.2 1.9 collective-permute-done.4
  20.5 149.1 %while.51 = (s32[]{:T(128)}, f32[2,3,4,256]{3,2,0,1:T(4,128)S(1)}, f32[2,27,3,4,256]{4,3,0,2,1:T(4,128)S(1)}, f32[2,27,4,256]{3,2,1,0:T(4,128)S(1)}, f32[2,3,4,2...) while((s32[]{:T(128)}, f32[2,3,4,256]{3,2,0,1:T(4,128)S(1)}, ...), condition=%wide.region_5.6_spmd.clone, body=%wide.region_0.5_spmd.sunk.clone.sunk | while | flops 7605253 | bytes 5263704 | solution.py:84
  20.6 74.4 %while.54 = (s32[]{:T(128)}, f32[3,4,256]{2,1,0:T(4,128)S(1)}, f32[27,4,256]{2,1,0:T(4,128)S(1)}, f32[27,3,4,256]{3,2,1,0:T(4,128)S(1)}, f32[3,4,256]{2,1,0:T(4,...) while((s32[]{:T(128)}, f32[3,4,256]{2,1,0:T(4,128)S(1)}, ...), condition=%wide.region_4.4_spmd.clone.clone, body=%wide.region_1.3_spmd.sunk.clone.clone.sunk | while | flops 7605251 | bytes 4329627 | solution.py:81
  22.4 0.9 multiply_reduce_fusion.11
  25.1 0.9 multiply_reduce_fusion.11
  36.2 0.9 multiply_reduce_fusion.11
  38.9 0.9 multiply_reduce_fusion.11
  41.7 0.9 multiply_reduce_fusion.11
  44.4 0.9 multiply_reduce_fusion.11
  47.2 0.9 multiply_reduce_fusion.11
  50.0 0.9 multiply_reduce_fusion.11
  52.7 0.9 multiply_reduce_fusion.11
  61.0 0.9 multiply_reduce_fusion.11
  95.2 74.4 %while.54 = (s32[]{:T(128)}, f32[3,4,256]{2,1,0:T(4,128)S(1)}, f32[27,4,256]{2,1,0:T(4,128)S(1)}, f32[27,3,4,256]{3,2,1,0:T(4,128)S(1)}, f32[3,4,256]{2,1,0:T(4,...) while((s32[]{:T(128)}, f32[3,4,256]{2,1,0:T(4,128)S(1)}, ...), condition=%wide.region_4.4_spmd.clone.clone, body=%wide.region_1.3_spmd.sunk.clone.clone.sunk | while | flops 7605251 | bytes 4329627 | solution.py:81
  170.3 1.5 collective-permute-start.7
  171.8 1.7 collective-permute-done.6
  174.1 1.4 collective-permute-start.8
  175.5 2.5 collective-permute-start.9
  178.1 1.6 collective-permute-done.8
  180.5 1.3 collective-permute-done.11
  181.9 2.4 collective-permute-done.10
  184.4 1.0 stack.12
  185.9 149.1 %while.53 = (s32[]{:T(128)}, f32[2,3,4,256]{3,2,0,1:T(4,128)S(1)}, f32[2,27,3,4,256]{4,3,2,1,0:T(4,128)S(1)}, f32[2,27,4,256]{3,2,1,0:T(4,128)S(1)}, f32[2,3,4,2...) while((s32[]{:T(128)}, f32[2,3,4,256]{3,2,0,1:T(4,128)S(1)}, ...), condition=%wide.region_11.12_spmd.clone, body=%wide.region_6.11_spmd.sunk.clone.sunk | while | flops 7605253 | bytes 5263704 | solution.py:84
  186.0 74.4 %while.55 = (s32[]{:T(128)}, f32[3,4,256]{2,1,0:T(4,128)S(1)}, f32[27,4,256]{2,1,0:T(4,128)S(1)}, f32[27,3,4,256]{3,2,1,0:T(4,128)S(1)}, f32[3,4,256]{2,1,0:T(4,...) while((s32[]{:T(128)}, f32[3,4,256]{2,1,0:T(4,128)S(1)}, ...), condition=%wide.region_10.10_spmd.clone.clone, body=%wide.region_7.9_spmd.sunk.clone.clone.sunk | while | flops 7605251 | bytes 4329627 | solution.py:81
  260.5 74.4 %while.55 = (s32[]{:T(128)}, f32[3,4,256]{2,1,0:T(4,128)S(1)}, f32[27,4,256]{2,1,0:T(4,128)S(1)}, f32[27,3,4,256]{3,2,1,0:T(4,128)S(1)}, f32[3,4,256]{2,1,0:T(4,...) while((s32[]{:T(128)}, f32[3,4,256]{2,1,0:T(4,128)S(1)}, ...), condition=%wide.region_10.10_spmd.clone.clone, body=%wide.region_7.9_spmd.sunk.clone.clone.sunk | while | flops 7605251 | bytes 4329627 | solution.py:81
  (856 shorter events, 290.2 us)
Async XLA Ops:
  2.2 4.8 %collective-permute-start = (f32[4,1,4,1,256]{4,2,1,0,3:T(4,128)S(1)}, f32[4,1,4,1,256]{4,2,1,0,3:T(4,128)S(1)}, u32[]{:S(2)}, u32[]{:S(2)}) collective-permute-start(f32[4,1,4,1,256]{4,2,1,0,3:T(4,128)S(1)} %get-tuple-element.338), channel_id=1, source_target_pairs={{0,16},{16,0},{1,17},{17,1},{2,18},{18,2},{3,19},{19,3},{4,20},{20... | collective-permute-start | bytes 49160 | tf_op jit(solution)/shard_map/ppermute | solution.py:16
  5.2 3.7 %collective-permute-start.1 = (f32[4,1,4,1,256]{4,2,1,0,3:T(4,128)S(1)}, f32[4,1,4,1,256]{4,2,1,0,3:T(4,128)S(1)}, u32[]{:S(2)}, u32[]{:S(2)}) collective-permute-start(f32[4,1,4,1,256]{4,2,1,0,3:T(4,128)S(1)} %get-tuple-element.339), channel_id=1, source_target_pairs={{16,0},{0,16},{17,1},{1,17},{18,2},{2,18},{19,3},{3,19},{20,4},{4,... | collective-permute-start | bytes 49160 | tf_op jit(solution)/shard_map/ppermute | solution.py:19
  9.0 5.6 %collective-permute-start.2 = (f32[4,4,1,1,256]{4,2,1,0,3:T(1,128)S(1)}, f32[4,4,1,1,256]{4,2,1,0,3:T(1,128)S(1)}, u32[]{:S(2)}, u32[]{:S(2)}) collective-permute-start(f32[4,4,1,1,256]{4,2,1,0,3:T(1,128)S(1)} %get-tuple-element.326), channel_id=1, source_target_pairs={{0,4},{4,8},{8,12},{12,0},{1,5},{5,9},{9,13},{13,1},{2,6},{6,10},{... | collective-permute-start | bytes 49160 | tf_op jit(solution)/shard_map/ppermute | solution.py:16
  10.6 9.6 %copy-start = (f32[3,2,4,1,256]{4,3,2,1,0:T(1,128)S(1)}, f32[3,2,4,1,256]{4,3,2,1,0:T(1,128)}, u32[]{:S(2)}) copy-start(f32[3,2,4,1,256]{4,3,2,1,0:T(1,128)} %param.14) | copy-start | bytes 73732
  10.6 4.0 %collective-permute-start.3 = (f32[4,4,1,1,256]{4,2,1,0,3:T(1,128)S(1)}, f32[4,4,1,1,256]{4,2,1,0,3:T(1,128)S(1)}, u32[]{:S(2)}, u32[]{:S(2)}) collective-permute-start(f32[4,4,1,1,256]{4,2,1,0,3:T(1,128)S(1)} %get-tuple-element.327), channel_id=1, source_target_pairs={{4,0},{8,4},{12,8},{0,12},{5,1},{9,5},{13,9},{1,13},{6,2},{10,6},{... | collective-permute-start | bytes 49160 | tf_op jit(solution)/shard_map/ppermute | solution.py:19
  14.6 4.4 %collective-permute-start.4 = (f32[4,4,6,1,256]{4,2,1,0,3:T(8,128)S(1)}, f32[4,4,6,1,256]{4,2,1,0,3:T(8,128)S(1)}, u32[]{:S(2)}, u32[]{:S(2)}) collective-permute-start(f32[4,4,6,1,256]{4,2,1,0,3:T(8,128)S(1)} %get-tuple-element.307), channel_id=1, source_target_pairs={{0,1},{1,2},{2,3},{3,0},{4,5},{5,6},{6,7},{7,4},{8,9},{9,10},{10,1... | collective-permute-start | bytes 294920 | tf_op jit(solution)/shard_map/ppermute | solution.py:16
  14.7 4.8 %collective-permute-start.5 = (f32[4,4,6,1,256]{4,2,1,3,0:T(8,128)S(1)}, f32[4,4,6,1,256]{4,2,1,3,0:T(8,128)S(1)}, u32[]{:S(2)}, u32[]{:S(2)}) collective-permute-start(f32[4,4,6,1,256]{4,2,1,3,0:T(8,128)S(1)} %get-tuple-element.306), channel_id=1, source_target_pairs={{1,0},{2,1},{3,2},{0,3},{5,4},{6,5},{7,6},{4,7},{9,8},{10,9},{11,1... | collective-permute-start | bytes 294920 | tf_op jit(solution)/shard_map/ppermute | solution.py:19
  20.5 149.2 %copy-start.1 = (f32[3,2,4,1,256]{4,3,2,1,0:T(1,128)S(1)}, f32[3,2,4,1,256]{4,3,2,1,0:T(1,128)}, u32[]{:S(2)}) copy-start(f32[3,2,4,1,256]{4,3,2,1,0:T(1,128)} %param.15) | copy-start | bytes 73732
  169.7 3.8 %collective-permute-start.6 = (f32[3,1,4,1,256]{4,3,2,1,0:T(1,128)S(1)}, f32[3,1,4,1,256]{4,3,2,1,0:T(1,128)S(1)}, u32[]{:S(2)}, u32[]{:S(2)}) collective-permute-start(f32[3,1,4,1,256]{4,3,2,1,0:T(1,128)S(1)} %get-tuple-element.342), channel_id=1, source_target_pairs={{0,16},{16,0},{1,17},{17,1},{2,18},{18,2},{3,19},{19,3},{4,20},{20... | collective-permute-start | bytes 36872 | tf_op jit(solution)/shard_map/ppermute | solution.py:16
  170.3 3.8 %collective-permute-start.7 = (f32[3,1,4,1,256]{4,3,2,1,0:T(1,128)S(1)}, f32[3,1,4,1,256]{4,3,2,1,0:T(1,128)S(1)}, u32[]{:S(2)}, u32[]{:S(2)}) collective-permute-start(f32[3,1,4,1,256]{4,3,2,1,0:T(1,128)S(1)} %get-tuple-element.343), channel_id=1, source_target_pairs={{16,0},{0,16},{17,1},{1,17},{18,2},{2,18},{19,3},{3,19},{20,4},{4,... | collective-permute-start | bytes 36872 | tf_op jit(solution)/shard_map/ppermute | solution.py:19
  174.1 5.6 %collective-permute-start.8 = (f32[3,4,1,1,256]{4,3,2,1,0:T(1,128)S(1)}, f32[3,4,1,1,256]{4,3,2,1,0:T(1,128)S(1)}, u32[]{:S(2)}, u32[]{:S(2)}) collective-permute-start(f32[3,4,1,1,256]{4,3,2,1,0:T(1,128)S(1)} %get-tuple-element.336), channel_id=1, source_target_pairs={{0,4},{4,8},{8,12},{12,0},{1,5},{5,9},{9,13},{13,1},{2,6},{6,10},{... | collective-permute-start | bytes 36872 | tf_op jit(solution)/shard_map/ppermute | solution.py:16
  175.5 4.1 %collective-permute-start.9 = (f32[3,4,1,1,256]{4,3,2,1,0:T(1,128)S(1)}, f32[3,4,1,1,256]{4,3,2,1,0:T(1,128)S(1)}, u32[]{:S(2)}, u32[]{:S(2)}) collective-permute-start(f32[3,4,1,1,256]{4,3,2,1,0:T(1,128)S(1)} %get-tuple-element.337), channel_id=1, source_target_pairs={{4,0},{8,4},{12,8},{0,12},{5,1},{9,5},{13,9},{1,13},{6,2},{10,6},{... | collective-permute-start | bytes 36872 | tf_op jit(solution)/shard_map/ppermute | solution.py:19
  179.8 2.0 collective-permute-start.11
  179.8 4.5 %collective-permute-start.10 = (f32[3,4,6,1,256]{4,3,2,1,0:T(1,128)S(1)}, f32[3,4,6,1,256]{4,3,2,1,0:T(1,128)S(1)}, u32[]{:S(2)}, u32[]{:S(2)}) collective-permute-start(f32[3,4,6,1,256]{4,3,2,1,0:T(1,128)S(1)} %pad_maximum_fusion.3), channel_id=1, source_target_pairs={{0,1},{1,2},{2,3},{3,0},{4,5},{5,6},{6,7},{7,4},{8,9},{9,10},{10,1... | collective-permute-start | bytes 221192 | tf_op jit(solution)/shard_map/ppermute | solution.py:16
where the time goes:
time: 340 us; the launch traced here: 336 us
  other arithmetic  217 us (64%)
  local copies, waits for them, and re-layouts  81.5 us (24%)
  starting transfers between devices  15.4 us (5%)
  waiting for transfers between devices  15.3 us (4%)
  loops' own time  5.74 us (2%)
    reduce_sum x108, other arithmetic, pair_tile(): return jnp.sum(scaled[None] * dist, axis=-1)  102 us
    add x108, local copies, waits for them, and re-layouts, pair_tile(): dist = dist + shift.reshape((3,) + (1,) * (dist.ndim - 1))  75.5 us
    mul x108, other arithmetic, pair_tile(): scaled = source_mass[..., None, :] * factor  59.1 us
    reduce_sum x108, other arithmetic, pair_tile(): square = jnp.sum(dist * dist, axis=0)  51.7 us
    ppermute x6, waiting for transfers between devices, with_halo(): lax.ppermute(lax.slice_in_dim(block, block.shape[dim] - width, None, axis...  10.9 us
    ppermute x6, starting transfers between devices, with_halo(): lax.ppermute(lax.slice_in_dim(block, 0, width, axis=dim), axis, backward)  8.14 us
    ppermute x6, starting transfers between devices, with_halo(): lax.ppermute(lax.slice_in_dim(block, block.shape[dim] - width, None, axis...  7.22 us
  transfers between devices with their start and end apart: 12, of which 10 were waited for; matrix products, arithmetic and copies ran while one was open for 0% of the time, Pallas kernels for 0%

commit v1 on v0

v1 whole, which is shorter than its diff:
```python
import functools

import jax
import jax.numpy as jnp
from jax import lax
from jax.experimental import pallas as pl
from jax.experimental.pallas import tpu as pltpu
from jax.sharding import PartitionSpec as P

SUBSTEPS = 2
WIDE = 256


def with_halo(block, sides, width):
    for axis, dim in sides:
        count = lax.axis_size(axis)
        forward = [(i, i + 1) for i in range(count - 1)]
        forward.append((count - 1, 0))
        backward = [(target, source) for source, target in forward]
        low = lax.ppermute(
            lax.slice_in_dim(block, block.shape[dim] - width, None, axis=dim), axis, forward
        )
        high = lax.ppermute(lax.slice_in_dim(block, 0, width, axis=dim), axis, backward)
        block = jnp.concatenate([low, block, high], axis=dim)
    return block


def split3(tile):
    high = tile.astype(jnp.bfloat16).astype(jnp.float32)
    rest = tile - high
    mid = rest.astype(jnp.bfloat16).astype(jnp.float32)
    return high, mid, rest - mid


def force_kernel(span, counts, src, vel, pos_out, vel_out, pack, tfeat, dist_a, dist_b, acc):
    span_x, span_y, span_z = span
    slots = src.shape[-1]
    row8 = lax.broadcasted_iota(jnp.int32, (8, WIDE), 0)
    lane128 = lax.broadcasted_iota(jnp.int32, (4, 128), 1)
    row4 = lax.broadcasted_iota(jnp.int32, (4, slots), 0)
    pad = 128 - 48
    pack[...] = jnp.zeros_like(pack)

    def one_leaf(leaf, carry):
        at_x = leaf // (span_y * span_z)
        at_y = (leaf // span_z) % span_y
        at_z = leaf % span_z

        def put(tile, off):
            start = pl.multiple_of((off // 128) * 128, 128)
            shift = off % 128
            wide = jnp.concatenate([tile, jnp.zeros((4, 128), jnp.float32)], axis=1)
            wide = pltpu.roll(wide, shift, 1)
            old = pack[0:4, pl.ds(start, 128)]
            pack[0:4, pl.ds(start, 128)] = jnp.where(lane128 < shift, old, wide[:, :128])
            pack[0:4, pl.ds(start + 128, slots)] = wide[:, 128:]

        def one_source(k, off):
            step_x = k // 9
            step_y = (k // 3) % 3
            step_z = k % 3
            tile = src[at_x + step_x, at_y + step_y, at_z + step_z]
            move = jnp.where(
                row4 == 0,
                (step_x - 1).astype(jnp.float32) - 0.5,
                jnp.where(
                    row4 == 1,
                    (step_y - 1).astype(jnp.float32) - 0.5,
                    jnp.where(row4 == 2, (step_z - 1).astype(jnp.float32) - 0.5, 0.0),
                ),
            )
            put(tile + move, off)
            place = ((at_x + step_x) * (span_y + 2) + at_y + step_y) * (span_z + 2) + at_z + step_z
            return off + counts[place]

        total = lax.fori_loop(0, 27, one_source, jnp.int32(0))
        put(jnp.zeros((4, slots), jnp.float32), total)
        pack[0:4, pl.ds(pl.multiple_of((total // 128) * 128, 128) + 384, 2 * WIDE)] = jnp.zeros(
            (4, 2 * WIDE), jnp.float32
        )

        own = src[at_x + 1, at_y + 1, at_z + 1]
        own = jnp.concatenate([own, jnp.zeros((4, slots), jnp.float32)], axis=0)
        rows = lax.broadcasted_iota(jnp.int32, (8, slots), 0)
        centred = jnp.where(rows < 3, own - 0.5, 0.0)
        norm = jnp.sum(centred * centred, axis=0, keepdims=True) + 0.01
        high, mid, low = split3(jnp.where(rows == 4, norm, -2.0 * centred))
        high = high + jnp.where(rows == 3, 1.0, 0.0)
        feats = jnp.concatenate(
            [high, mid, high, mid, low, high, jnp.zeros((pad, slots), jnp.float32)], axis=0
        )
        tfeat[...] = feats.T.astype(jnp.bfloat16)
        acc[...] = jnp.zeros_like(acc)

        def distances(chunk):
            tile = pack[:, pl.ds(pl.multiple_of(chunk * WIDE, WIDE), WIDE)]
            where = jnp.where(row8 < 3, tile, 0.0)
            square = jnp.sum(where * where, axis=0, keepdims=True)
            high, mid, low = split3(
                jnp.where(row8 == 3, square, jnp.where(row8 == 4, 1.0, where))
            )
            feats = jnp.concatenate(
                [high, high, mid, mid, high, low, jnp.zeros((pad, WIDE), jnp.float32)], axis=0
            ).astype(jnp.bfloat16)
            return jnp.dot(tfeat[...], feats, preferred_element_type=jnp.float32)

        def gather(chunk, dist):
            tile = pack[:, pl.ds(pl.multiple_of(chunk * WIDE, WIDE), WIDE)]
            mass = tile[3:4, :]
            terms = [
                jnp.broadcast_to(tile[0:1, :] * mass, (8, WIDE)),
                jnp.broadcast_to(tile[1:2, :] * mass, (8, WIDE)),
                jnp.broadcast_to(tile[2:3, :] * mass, (8, WIDE)),
                jnp.broadcast_to(mass, (8, WIDE)),
            ]
            for group in range(slots // 8):
                spot = slice(8 * group, 8 * group + 8)
                square = dist[spot, :]
                inverse = lax.rsqrt(square)
                edge = jnp.maximum(1.01 - square, 0.0) * inverse
                weight = edge * edge * inverse
                for comp in range(4):
                    part = weight * terms[comp]
                    acc[comp, spot, :] += part[:, :128] + part[:, 128:]

        dist_a[...] = distances(0)

        def two_chunks(pair, carry):
            dist_b[...] = distances(2 * pair + 1)
            gather(2 * pair, dist_a)
            dist_a[...] = distances(2 * pair + 2)
            gather(2 * pair + 1, dist_b)
            return carry

        lax.fori_loop(0, (total + 2 * WIDE - 1) // (2 * WIDE), two_chunks, 0)

        sums = [jnp.sum(acc[comp].T, axis=0, keepdims=True) for comp in range(4)]
        for comp in range(3):
            here = centred[comp : comp + 1]
            pull = sums[comp] - here * sums[3]
            speed = vel[leaf, comp : comp + 1, :] + 0.1 * pull
            vel_out[leaf, comp : comp + 1, :] = speed
            pos_out[leaf, comp : comp + 1, :] = own[comp : comp + 1] + 0.1 * speed
        return carry

    lax.fori_loop(0, span_x * span_y * span_z, one_leaf, 0)


def substep(span, counts, src, vel):
    leaves = span[0] * span[1] * span[2]
    slots = src.shape[-1]
    room = 27 * slots + 4 * WIDE + 512
    vmem = pl.BlockSpec(memory_space=pltpu.VMEM)
    return pl.pallas_call(
        functools.partial(force_kernel, span),
        out_shape=(
            jax.ShapeDtypeStruct((leaves, 3, slots), jnp.float32),
            jax.ShapeDtypeStruct((leaves, 3, slots), jnp.float32),
        ),
        in_specs=[pl.BlockSpec(memory_space=pltpu.SMEM), vmem, vmem],
        out_specs=(vmem, vmem),
        scratch_shapes=[
            pltpu.VMEM((8, room), jnp.float32),
            pltpu.VMEM((slots, 128), jnp.bfloat16),
            pltpu.VMEM((slots, WIDE), jnp.float32),
            pltpu.VMEM((slots, WIDE), jnp.float32),
            pltpu.VMEM((4, slots, 128), jnp.float32),
        ],
        name="forces",
    )(counts, src, vel)


def shards(offsets, velocity, mass, counts):
    slots = mass.shape[-1]
    span = mass.shape[:3]
    sides = (("gz", 2), ("gy", 1), ("gx", 0))
    slot = jnp.arange(slots, dtype=jnp.int32)
    weight = jnp.where(slot < counts[..., None], mass, jnp.float32(0.0))
    position = jnp.moveaxis(offsets, 0, 3)
    speed = jnp.moveaxis(velocity, 0, 3).reshape(-1, 3, slots)
    padded = with_halo(jnp.concatenate([position, weight[..., None, :]], axis=3), sides, 1)
    padded_mass = padded[..., 3:, :]
    live = jnp.max(jnp.where(padded_mass[..., 0, :] > 0, slot + 1, 0), axis=-1).reshape(-1)
    for step in range(SUBSTEPS):
        if step > 0:
            padded = jnp.concatenate([with_halo(position, sides, 1), padded_mass], axis=3)
        position, speed = substep(span, live, padded, speed)
        position = position.reshape(span + (3, slots))
    back = lambda array: jnp.moveaxis(array.reshape(span + (3, slots)), 3, 0)
    return (back(position), back(speed))


def solution(mesh):
    return jax.shard_map(
        shards,
        mesh=mesh,
        in_specs=(
            P(None, "gx", "gy", "gz", None),
            P(None, "gx", "gy", "gz", None),
            P("gx", "gy", "gz", None),
            P("gx", "gy", "gz"),
        ),
        out_specs=(P(None, "gx", "gy", "gz", None), P(None, "gx", "gy", "gz", None)),
        check_vma=False,
    )
```

time: 340 us -> 136 us (0.40); the launches traced: 336 us -> 136 us
  other arithmetic: 217 us -> 2.36 us
  Pallas kernels: 0 us -> 96 us
  local copies, waits for them, and re-layouts: 81.5 us -> 5.33 us
  loops' own time: 5.74 us -> 0 us
    reduce_sum x216 -> x0, other arithmetic: 154 us -> none  [the longest x108 102 us: pair_tile(): return jnp.sum(scaled[None] * dist, axis=-1)]
    pallas_call x0 -> x2, Pallas kernels: none -> 96 us  [substep(): pl.pallas_call(functools.partial(force_kernel, span), out_shape=(jax.Shap...]
    add x108 -> x0, local copies, waits for them, and re-layouts: 75.5 us -> none  [pair_tile(): dist = dist + shift.reshape((3,) + (1,) * (dist.ndim - 1))]
    mul x110 -> x0, other arithmetic: 59.1 us -> none  [the longest x108 59.1 us: pair_tile(): scaled = source_mass[..., None, :] * factor]
    another operation x6 -> x0, loops' own time: 5.74 us -> none  [the longest x4 5.51 us: one_block(): lax.scan(one_offset, jnp.zeros_like(target), (source_pos, source_mass, sh...]
  transfers between devices with their start and end apart: 12 -> 12, of which waited for: 10 -> 10; matrix products, arithmetic and copies ran while one was open for 0% -> 1% of each run, Pallas kernels for 0% -> 0%
where the time goes in v1:
time: 136 us
  Pallas kernels  96 us (71%)
  waiting for transfers between devices  16.4 us (12%)
  starting transfers between devices  15.6 us (11%)
  local copies, waits for them, and re-layouts  5.33 us (4%)
  other arithmetic  2.36 us (2%)
    pallas_call x2, Pallas kernels, substep(): pl.pallas_call(functools.partial(force_kernel, span), out_shape=(jax.Shap...  96 us
    ppermute x6, waiting for transfers between devices, with_halo(): lax.ppermute(lax.slice_in_dim(block, block.shape[dim] - width, None, axis...  9.79 us
    ppermute x6, starting transfers between devices, with_halo(): lax.ppermute(lax.slice_in_dim(block, 0, width, axis=dim), axis, backward)  9.5 us
    ppermute x6, waiting for transfers between devices, with_halo(): lax.ppermute(lax.slice_in_dim(block, 0, width, axis=dim), axis, backward)  6.57 us
    ppermute x6, starting transfers between devices, with_halo(): lax.ppermute(lax.slice_in_dim(block, block.shape[dim] - width, None, axis...  6.14 us
  transfers between devices with their start and end apart: 12, of which 10 were waited for; matrix products, arithmetic and copies ran while one was open for 1% of the time, Pallas kernels for 0%

profile of v1, /device:TPU:0, one launch (start us, length us, event | category | flops | bytes accessed | tf_op | source)
XLA Modules:
  0.0 136.5 jit_solution(4602013307542700322)
XLA Ops:
  0.6 0.8 copy.32
  1.4 0.7 copy-done.4
  2.2 2.5 %collective-permute-start.1 = (f32[2,4,1,4,256]{4,3,2,1,0:T(4,128)S(1)}, f32[2,4,1,4,256]{4,3,2,1,0:T(4,128)S(1)}, u32[]{:S(2)}, u32[]{:S(2)}) collective-permute-start(f32[2,4,1,4,256]{4,3,2,1,0:T(4,128)S(1)} %pad_maximum_fusion.4), channel_id=1, source_target_pairs={{1,0},{2,1},{3,2},{0,3},{5,4},{6,5},{7,6},{4,7},{9,8},{10,9},{11,1... | collective-permute-start | bytes 98312 | tf_op jit(solution)/shard_map/ppermute | solution.py:23
  4.7 1.7 %collective-permute-done.1 = f32[2,4,1,4,256]{4,3,2,1,0:T(4,128)S(1)} collective-permute-done((f32[2,4,1,4,256]{4,3,2,1,0:T(4,128)S(1)}, f32[2,4,1,4,256]{4,3,2,1,0:T(4,128)S(1)}, u32[]{:S(2)}, u32[]{:S(2)}) %collective-permute-start.1) | collective-permute-done | bytes 32800 | tf_op jit(solution)/shard_map/ppermute | solution.py:23
  6.4 1.6 %collective-permute-done = f32[2,4,1,4,256]{4,3,2,1,0:T(4,128)S(1)} collective-permute-done((f32[2,4,1,4,256]{4,3,2,1,0:T(4,128)S(1)}, f32[2,4,1,4,256]{4,3,2,1,0:T(4,128)S(1)}, u32[]{:S(2)}, u32[]{:S(2)}) %collective-permute-start) | collective-permute-done | bytes 32800 | tf_op jit(solution)/shard_map/ppermute | solution.py:20
  8.0 1.6 %collective-permute-start.2 = (f32[2,1,3,4,256]{4,3,2,1,0:T(4,128)S(1)}, f32[2,1,3,4,256]{4,3,2,1,0:T(4,128)S(1)}, u32[]{:S(2)}, u32[]{:S(2)}) collective-permute-start(f32[2,1,3,4,256]{4,3,2,1,0:T(4,128)S(1)} %get-tuple-element.14), channel_id=1, source_target_pairs={{0,4},{4,8},{8,12},{12,0},{1,5},{5,9},{9,13},{13,1},{2,6},{6,10},{... | collective-permute-start | bytes 73736 | tf_op jit(solution)/shard_map/ppermute | solution.py:20
  9.7 2.2 %collective-permute-start.3 = (f32[2,1,3,4,256]{4,3,2,1,0:T(4,128)S(1)}, f32[2,1,3,4,256]{4,3,2,1,0:T(4,128)S(1)}, u32[]{:S(2)}, u32[]{:S(2)}) collective-permute-start(f32[2,1,3,4,256]{4,3,2,1,0:T(4,128)S(1)} %get-tuple-element.15), channel_id=1, source_target_pairs={{4,0},{8,4},{12,8},{0,12},{5,1},{9,5},{13,9},{1,13},{6,2},{10,6},{... | collective-permute-start | bytes 73736 | tf_op jit(solution)/shard_map/ppermute | solution.py:23
  11.9 0.6 copy.25
  12.5 1.2 collective-permute-done.2
  13.8 1.6 %collective-permute-start.4 = (f32[1,6,3,4,256]{4,3,2,1,0:T(4,128)S(1)}, f32[1,6,3,4,256]{4,3,2,1,0:T(4,128)S(1)}, u32[]{:S(2)}, u32[]{:S(2)}) collective-permute-start(f32[1,6,3,4,256]{4,3,2,1,0:T(4,128)S(1)} %get-tuple-element.12), channel_id=1, source_target_pairs={{0,16},{16,0},{1,17},{17,1},{2,18},{18,2},{3,19},{19,3},{4,20},{20... | collective-permute-start | bytes 221192 | tf_op jit(solution)/shard_map/ppermute | solution.py:20
  15.4 0.5 collective-permute-start.5
  15.9 2.3 %collective-permute-done.4 = f32[1,6,3,4,256]{4,3,2,1,0:T(4,128)S(1)} collective-permute-done((f32[1,6,3,4,256]{4,3,2,1,0:T(4,128)S(1)}, f32[1,6,3,4,256]{4,3,2,1,0:T(4,128)S(1)}, u32[]{:S(2)}, u32[]{:S(2)}) %collective-permute-start.4) | collective-permute-done | bytes 73760 | tf_op jit(solution)/shard_map/ppermute | solution.py:20
  18.3 1.5 %collective-permute-done.5 = f32[1,6,3,4,256]{4,3,2,1,0:T(4,128)S(1)} collective-permute-done((f32[1,6,3,4,256]{4,3,2,1,0:T(4,128)S(1)}, f32[1,6,3,4,256]{4,3,2,1,0:T(4,128)S(1)}, u32[]{:S(2)}, u32[]{:S(2)}) %collective-permute-start.5) | collective-permute-done | bytes 73760 | tf_op jit(solution)/shard_map/ppermute | solution.py:23
  20.0 0.4 select_reduce_fusion
  20.4 0.1 copy.24
  20.5 0.6 reshape.32.counts
  21.1 48.0 %forces.2 = (f32[8,3,256]{2,1,0:T(4,128)}, f32[8,3,256]{2,1,0:T(4,128)}) custom-call(s32[72]{0:T(128)} %reshape.32.counts, f32[4,6,3,4,256]{4,3,2,1,0:T(4,128)} %copy-done, f32[8,3,256]{2,1,0:T(4,128)} %bitcast.26), custom_call_target="tpu_custom_call" | custom-call | tf_op jit(solution)/shard_map/forces/pallas_call | solution.py:154
  69.1 0.5 collective-permute-start.6
  69.6 1.5 %collective-permute-done.7 = f32[2,4,1,3,256]{4,3,2,1,0:T(4,128)S(1)} collective-permute-done((f32[2,4,1,3,256]{4,3,2,1,0:T(4,128)}, f32[2,4,1,3,256]{4,3,2,1,0:T(4,128)S(1)}, u32[]{:S(2)}, u32[]{:S(2)}) %collective-permute-start.7) | collective-permute-done | bytes 24608 | tf_op jit(solution)/shard_map/ppermute | solution.py:23
  71.1 1.6 %collective-permute-done.6 = f32[2,4,1,3,256]{4,3,2,1,0:T(4,128)S(1)} collective-permute-done((f32[2,4,1,3,256]{4,3,2,1,0:T(4,128)}, f32[2,4,1,3,256]{4,3,2,1,0:T(4,128)S(1)}, u32[]{:S(2)}, u32[]{:S(2)}) %collective-permute-start.6) | collective-permute-done | bytes 24608 | tf_op jit(solution)/shard_map/ppermute | solution.py:20
  72.7 0.7 pad_maximum_fusion.7
  73.5 0.5 collective-permute-start.8
  74.0 4.1 %collective-permute-start.9 = (f32[2,1,3,3,256]{4,3,2,1,0:T(4,128)S(1)}, f32[2,1,3,3,256]{4,3,2,1,0:T(4,128)S(1)}, u32[]{:S(2)}, u32[]{:S(2)}) collective-permute-start(f32[2,1,3,3,256]{4,3,2,1,0:T(4,128)S(1)} %get-tuple-element.17), channel_id=1, source_target_pairs={{4,0},{8,4},{12,8},{0,12},{5,1},{9,5},{13,9},{1,13},{6,2},{10,6},{... | collective-permute-start | bytes 55304 | tf_op jit(solution)/shard_map/ppermute | solution.py:23
  78.0 1.7 %collective-permute-done.8 = f32[2,1,3,3,256]{4,3,2,1,0:T(4,128)S(1)} collective-permute-done((f32[2,1,3,3,256]{4,3,2,1,0:T(4,128)S(1)}, f32[2,1,3,3,256]{4,3,2,1,0:T(4,128)S(1)}, u32[]{:S(2)}, u32[]{:S(2)}) %collective-permute-start.8) | collective-permute-done | bytes 18464 | tf_op jit(solution)/shard_map/ppermute | solution.py:20
  79.9 1.9 %collective-permute-start.10 = (f32[1,6,3,3,256]{4,3,2,1,0:T(4,128)S(1)}, f32[1,6,3,3,256]{4,3,2,1,0:T(4,128)S(1)}, u32[]{:S(2)}, u32[]{:S(2)}) collective-permute-start(f32[1,6,3,3,256]{4,3,2,1,0:T(4,128)S(1)} %get-tuple-element.10), channel_id=1, source_target_pairs={{0,16},{16,0},{1,17},{17,1},{2,18},{18,2},{3,19},{19,3},{4,20},{20... | collective-permute-start | bytes 165896 | tf_op jit(solution)/shard_map/ppermute | solution.py:20
  81.8 0.2 collective-permute-start.11
  82.0 1.0 slice.38
  83.0 1.3 collective-permute-done.10
  84.3 1.9 %collective-permute-done.11 = f32[1,6,3,3,256]{4,3,2,1,0:T(4,128)S(1)} collective-permute-done((f32[1,6,3,3,256]{4,3,2,1,0:T(4,128)S(1)}, f32[1,6,3,3,256]{4,3,2,1,0:T(4,128)S(1)}, u32[]{:S(2)}, u32[]{:S(2)}) %collective-permute-start.11) | collective-permute-done | bytes 55328 | tf_op jit(solution)/shard_map/ppermute | solution.py:23
  86.2 0.8 pad_maximum_fusion.1.src
  87.0 48.0 %forces.3 = (f32[8,3,256]{2,1,0:T(4,128)}, f32[8,3,256]{2,1,0:T(4,128)}) custom-call(s32[72]{0:T(128)} %reshape.32.counts, f32[4,6,3,4,256]{4,3,2,1,0:T(4,128)} %pad_maximum_fusion.1.src, f32[8,3,256]{2,1,0:T(4,128)} %get-tuple-element.7.vel), custom_call_target="tpu_custom_call" | custom-call | tf_op jit(solution)/shard_map/forces/pallas_call | solution.py:154
  135.0 1.4 %copy_bitcast_fusion.1 = (f32[3,2,4,1,256]{4,3,2,1,0:T(1,128)}, f32[3,2,4,1,256]{4,3,2,1,0:T(1,128)}) fusion(f32[2,4,1,3,256]{4,3,1,0,2:T(4,128)} %bitcast.28, f32[2,4,1,3,256]{4,3,1,0,2:T(4,128)} %bitcast.27), kind=kLoop, calls=%fused_computation.16 | loop fusion | bytes 98304 | tf_op jit(solution)/shard_map/transpose | solution.py:189
  (23 shorter events, 0.5 us)
Async XLA Ops:
  0.6 0.8 copy-start.3
  1.4 0.7 copy-start.4
  2.2 9.7 %copy-start.2 = (f32[3,2,4,1,256]{4,3,2,1,0:T(1,128)S(1)}, f32[3,2,4,1,256]{4,3,2,1,0:T(1,128)}, u32[]{:S(2)}) copy-start(f32[3,2,4,1,256]{4,3,2,1,0:T(1,128)} %param.5) | copy-start | bytes 73732
  2.2 4.2 %collective-permute-start.1 = (f32[2,4,1,4,256]{4,3,2,1,0:T(4,128)S(1)}, f32[2,4,1,4,256]{4,3,2,1,0:T(4,128)S(1)}, u32[]{:S(2)}, u32[]{:S(2)}) collective-permute-start(f32[2,4,1,4,256]{4,3,2,1,0:T(4,128)S(1)} %pad_maximum_fusion.4), channel_id=1, source_target_pairs={{1,0},{2,1},{3,2},{0,3},{5,4},{6,5},{7,6},{4,7},{9,8},{10,9},{11,1... | collective-permute-start | bytes 98312 | tf_op jit(solution)/shard_map/ppermute | solution.py:23
  4.7 3.3 %collective-permute-start = (f32[2,4,1,4,256]{4,3,2,1,0:T(4,128)S(1)}, f32[2,4,1,4,256]{4,3,2,1,0:T(4,128)S(1)}, u32[]{:S(2)}, u32[]{:S(2)}) collective-permute-start(f32[2,4,1,4,256]{4,3,2,1,0:T(4,128)S(1)} %pad_maximum_fusion.4), channel_id=1, source_target_pairs={{0,1},{1,2},{2,3},{3,0},{4,5},{5,6},{6,7},{7,4},{8,9},{9,10},{10,1... | collective-permute-start | bytes 98312 | tf_op jit(solution)/shard_map/ppermute | solution.py:20
  8.0 5.7 %collective-permute-start.2 = (f32[2,1,3,4,256]{4,3,2,1,0:T(4,128)S(1)}, f32[2,1,3,4,256]{4,3,2,1,0:T(4,128)S(1)}, u32[]{:S(2)}, u32[]{:S(2)}) collective-permute-start(f32[2,1,3,4,256]{4,3,2,1,0:T(4,128)S(1)} %get-tuple-element.14), channel_id=1, source_target_pairs={{0,4},{4,8},{8,12},{12,0},{1,5},{5,9},{9,13},{13,1},{2,6},{6,10},{... | collective-permute-start | bytes 73736 | tf_op jit(solution)/shard_map/ppermute | solution.py:20
  9.7 4.1 %collective-permute-start.3 = (f32[2,1,3,4,256]{4,3,2,1,0:T(4,128)S(1)}, f32[2,1,3,4,256]{4,3,2,1,0:T(4,128)S(1)}, u32[]{:S(2)}, u32[]{:S(2)}) collective-permute-start(f32[2,1,3,4,256]{4,3,2,1,0:T(4,128)S(1)} %get-tuple-element.15), channel_id=1, source_target_pairs={{4,0},{8,4},{12,8},{0,12},{5,1},{9,5},{13,9},{1,13},{6,2},{10,6},{... | collective-permute-start | bytes 73736 | tf_op jit(solution)/shard_map/ppermute | solution.py:23
  13.8 4.4 %collective-permute-start.4 = (f32[1,6,3,4,256]{4,3,2,1,0:T(4,128)S(1)}, f32[1,6,3,4,256]{4,3,2,1,0:T(4,128)S(1)}, u32[]{:S(2)}, u32[]{:S(2)}) collective-permute-start(f32[1,6,3,4,256]{4,3,2,1,0:T(4,128)S(1)} %get-tuple-element.12), channel_id=1, source_target_pairs={{0,16},{16,0},{1,17},{17,1},{2,18},{18,2},{3,19},{19,3},{4,20},{20... | collective-permute-start | bytes 221192 | tf_op jit(solution)/shard_map/ppermute | solution.py:20
  15.4 4.4 %collective-permute-start.5 = (f32[1,6,3,4,256]{4,3,2,1,0:T(4,128)S(1)}, f32[1,6,3,4,256]{4,3,2,1,0:T(4,128)S(1)}, u32[]{:S(2)}, u32[]{:S(2)}) collective-permute-start(f32[1,6,3,4,256]{4,3,2,1,0:T(4,128)S(1)} %get-tuple-element.13), channel_id=1, source_target_pairs={{16,0},{0,16},{17,1},{1,17},{18,2},{2,18},{19,3},{3,19},{20,4},{4,... | collective-permute-start | bytes 221192 | tf_op jit(solution)/shard_map/ppermute | solution.py:23
  19.8 1.3 copy-start
  69.1 10.7 %copy-start.1 = (f32[8,3,256]{2,1,0:T(4,128)S(1)}, f32[8,3,256]{2,1,0:T(4,128)}, u32[]{:S(2)}) copy-start(f32[8,3,256]{2,1,0:T(4,128)} %get-tuple-element.6) | copy-start | bytes 73732
  69.1 2.0 %collective-permute-start.7 = (f32[2,4,1,3,256]{4,3,2,1,0:T(4,128)}, f32[2,4,1,3,256]{4,3,2,1,0:T(4,128)S(1)}, u32[]{:S(2)}, u32[]{:S(2)}) collective-permute-start(f32[2,4,1,3,256]{4,3,2,1,0:T(4,128)} %bitcast.21), channel_id=1, source_target_pairs={{1,0},{2,1},{3,2},{0,3},{5,4},{6,5},{7,6},{4,7},{9,8},{10,9},{11,1... | collective-permute-start | bytes 73736 | tf_op jit(solution)/shard_map/ppermute | solution.py:23
  69.1 3.6 %collective-permute-start.6 = (f32[2,4,1,3,256]{4,3,2,1,0:T(4,128)}, f32[2,4,1,3,256]{4,3,2,1,0:T(4,128)S(1)}, u32[]{:S(2)}, u32[]{:S(2)}) collective-permute-start(f32[2,4,1,3,256]{4,3,2,1,0:T(4,128)} %bitcast.22), channel_id=1, source_target_pairs={{0,1},{1,2},{2,3},{3,0},{4,5},{5,6},{6,7},{7,4},{8,9},{9,10},{10,1... | collective-permute-start | bytes 73736 | tf_op jit(solution)/shard_map/ppermute | solution.py:20
  73.5 6.3 %collective-permute-start.8 = (f32[2,1,3,3,256]{4,3,2,1,0:T(4,128)S(1)}, f32[2,1,3,3,256]{4,3,2,1,0:T(4,128)S(1)}, u32[]{:S(2)}, u32[]{:S(2)}) collective-permute-start(f32[2,1,3,3,256]{4,3,2,1,0:T(4,128)S(1)} %get-tuple-element.16), channel_id=1, source_target_pairs={{0,4},{4,8},{8,12},{12,0},{1,5},{5,9},{9,13},{13,1},{2,6},{6,10},{... | collective-permute-start | bytes 55304 | tf_op jit(solution)/shard_map/ppermute | solution.py:20
  74.0 5.8 %collective-permute-start.9 = (f32[2,1,3,3,256]{4,3,2,1,0:T(4,128)S(1)}, f32[2,1,3,3,256]{4,3,2,1,0:T(4,128)S(1)}, u32[]{:S(2)}, u32[]{:S(2)}) collective-permute-start(f32[2,1,3,3,256]{4,3,2,1,0:T(4,128)S(1)} %get-tuple-element.17), channel_id=1, source_target_pairs={{4,0},{8,4},{12,8},{0,12},{5,1},{9,5},{13,9},{1,13},{6,2},{10,6},{... | collective-permute-start | bytes 55304 | tf_op jit(solution)/shard_map/ppermute | solution.py:23
  79.9 4.4 %collective-permute-start.10 = (f32[1,6,3,3,256]{4,3,2,1,0:T(4,128)S(1)}, f32[1,6,3,3,256]{4,3,2,1,0:T(4,128)S(1)}, u32[]{:S(2)}, u32[]{:S(2)}) collective-permute-start(f32[1,6,3,3,256]{4,3,2,1,0:T(4,128)S(1)} %get-tuple-element.10), channel_id=1, source_target_pairs={{0,16},{16,0},{1,17},{17,1},{2,18},{18,2},{3,19},{19,3},{4,20},{20... | collective-permute-start | bytes 165896 | tf_op jit(solution)/shard_map/ppermute | solution.py:20
  81.8 4.4 %collective-permute-start.11 = (f32[1,6,3,3,256]{4,3,2,1,0:T(4,128)S(1)}, f32[1,6,3,3,256]{4,3,2,1,0:T(4,128)S(1)}, u32[]{:S(2)}, u32[]{:S(2)}) collective-permute-start(f32[1,6,3,3,256]{4,3,2,1,0:T(4,128)S(1)} %get-tuple-element.11), channel_id=1, source_target_pairs={{16,0},{0,16},{17,1},{1,17},{18,2},{2,18},{19,3},{3,19},{20,4},{4,... | collective-permute-start | bytes 165896 | tf_op jit(solution)/shard_map/ppermute | solution.py:23

commit v2 on v1

--- a/solution.py
+++ b/solution.py
@@ -47,35 +47,30 @@
         at_z = leaf % span_z
 
         def put(tile, off):
-            start = pl.multiple_of((off // 128) * 128, 128)
-            shift = off % 128
+            shift = lax.bitwise_and(off, 127)
+            start = pl.multiple_of(off - shift, 128)
             wide = jnp.concatenate([tile, jnp.zeros((4, 128), jnp.float32)], axis=1)
             wide = pltpu.roll(wide, shift, 1)
             old = pack[0:4, pl.ds(start, 128)]
             pack[0:4, pl.ds(start, 128)] = jnp.where(lane128 < shift, old, wide[:, :128])
             pack[0:4, pl.ds(start + 128, slots)] = wide[:, 128:]
 
-        def one_source(k, off):
-            step_x = k // 9
-            step_y = (k // 3) % 3
-            step_z = k % 3
-            tile = src[at_x + step_x, at_y + step_y, at_z + step_z]
-            move = jnp.where(
-                row4 == 0,
-                (step_x - 1).astype(jnp.float32) - 0.5,
-                jnp.where(
-                    row4 == 1,
-                    (step_y - 1).astype(jnp.float32) - 0.5,
-                    jnp.where(row4 == 2, (step_z - 1).astype(jnp.float32) - 0.5, 0.0),
-                ),
-            )
-            put(tile + move, off)
-            place = ((at_x + step_x) * (span_y + 2) + at_y + step_y) * (span_z + 2) + at_z + step_z
-            return off + counts[place]
-
-        total = lax.fori_loop(0, 27, one_source, jnp.int32(0))
+        total = jnp.int32(0)
+        for step_x in range(3):
+            for step_y in range(3):
+                for step_z in range(3):
+                    move = jnp.where(
+                        row4 == 0,
+                        step_x - 1.5,
+                        jnp.where(
+                            row4 == 1, step_y - 1.5, jnp.where(row4 == 2, step_z - 1.5, 0.0)
+                        ),
+                    )
+                    put(src[at_x + step_x, at_y + step_y, at_z + step_z] + move, total)
+                    place = (at_x + step_x) * (span_y + 2) + at_y + step_y
+                    total = total + counts[place * (span_z + 2) + at_z + step_z]
         put(jnp.zeros((4, slots), jnp.float32), total)
-        pack[0:4, pl.ds(pl.multiple_of((total // 128) * 128, 128) + 384, 2 * WIDE)] = jnp.zeros(
+        pack[0:4, pl.ds(pl.multiple_of(total - lax.bitwise_and(total, 127), 128) + 384, 2 * WIDE)] = jnp.zeros(
             (4, 2 * WIDE), jnp.float32
         )
 

time: 136 us -> 104 us (0.76)
  Pallas kernels: 96 us -> 64.4 us
    pallas_call x2, Pallas kernels: 96 us -> 64.4 us  [substep(): pl.pallas_call(functools.partial(force_kernel, span), out_shape=(jax.Shap...]
  transfers between devices with their start and end apart: 12 -> 12, of which waited for: 10 -> 10; matrix products, arithmetic and copies ran while one was open for 1% -> 2% of each run, Pallas kernels for 0% -> 0%
where the time goes in v2:
time: 104 us
  Pallas kernels  64.4 us (62%)
  waiting for transfers between devices  16.1 us (15%)
  starting transfers between devices  14.9 us (14%)
  local copies, waits for them, and re-layouts  5.33 us (5%)
  other arithmetic  2.36 us (2%)
    pallas_call x2, Pallas kernels, substep(): pl.pallas_call(functools.partial(force_kernel, span), out_shape=(jax.Shap...  64.4 us
    ppermute x6, waiting for transfers between devices, with_halo(): lax.ppermute(lax.slice_in_dim(block, block.shape[dim] - width, None, axis...  10.1 us
    ppermute x6, starting transfers between devices, with_halo(): lax.ppermute(lax.slice_in_dim(block, 0, width, axis=dim), axis, backward)  8.84 us
    ppermute x6, starting transfers between devices, with_halo(): lax.ppermute(lax.slice_in_dim(block, block.shape[dim] - width, None, axis...  6.09 us
    ppermute x6, waiting for transfers between devices, with_halo(): lax.ppermute(lax.slice_in_dim(block, 0, width, axis=dim), axis, backward)  6.02 us
  transfers between devices with their start and end apart: 12, of which 10 were waited for; matrix products, arithmetic and copies ran while one was open for 2% of the time, Pallas kernels for 0%

profile of v2, /device:TPU:0, one launch (start us, length us, event | category | flops | bytes accessed | tf_op | source)
XLA Modules:
  0.0 103.8 jit_solution(12649478806903024820)
XLA Ops:
  0.6 0.8 copy.32
  1.4 0.7 copy-done.4
  2.2 2.5 %collective-permute-start.1 = (f32[2,4,1,4,256]{4,3,2,1,0:T(4,128)S(1)}, f32[2,4,1,4,256]{4,3,2,1,0:T(4,128)S(1)}, u32[]{:S(2)}, u32[]{:S(2)}) collective-permute-start(f32[2,4,1,4,256]{4,3,2,1,0:T(4,128)S(1)} %pad_maximum_fusion.4), channel_id=1, source_target_pairs={{1,0},{2,1},{3,2},{0,3},{5,4},{6,5},{7,6},{4,7},{9,8},{10,9},{11,1... | collective-permute-start | bytes 98312 | tf_op jit(solution)/shard_map/ppermute | solution.py:23
  4.7 1.7 %collective-permute-done.1 = f32[2,4,1,4,256]{4,3,2,1,0:T(4,128)S(1)} collective-permute-done((f32[2,4,1,4,256]{4,3,2,1,0:T(4,128)S(1)}, f32[2,4,1,4,256]{4,3,2,1,0:T(4,128)S(1)}, u32[]{:S(2)}, u32[]{:S(2)}) %collective-permute-start.1) | collective-permute-done | bytes 32800 | tf_op jit(solution)/shard_map/ppermute | solution.py:23
  6.4 1.6 %collective-permute-done = f32[2,4,1,4,256]{4,3,2,1,0:T(4,128)S(1)} collective-permute-done((f32[2,4,1,4,256]{4,3,2,1,0:T(4,128)S(1)}, f32[2,4,1,4,256]{4,3,2,1,0:T(4,128)S(1)}, u32[]{:S(2)}, u32[]{:S(2)}) %collective-permute-start) | collective-permute-done | bytes 32800 | tf_op jit(solution)/shard_map/ppermute | solution.py:20
  8.0 1.6 %collective-permute-start.2 = (f32[2,1,3,4,256]{4,3,2,1,0:T(4,128)S(1)}, f32[2,1,3,4,256]{4,3,2,1,0:T(4,128)S(1)}, u32[]{:S(2)}, u32[]{:S(2)}) collective-permute-start(f32[2,1,3,4,256]{4,3,2,1,0:T(4,128)S(1)} %get-tuple-element.14), channel_id=1, source_target_pairs={{0,4},{4,8},{8,12},{12,0},{1,5},{5,9},{9,13},{13,1},{2,6},{6,10},{... | collective-permute-start | bytes 73736 | tf_op jit(solution)/shard_map/ppermute | solution.py:20
  9.7 2.2 %collective-permute-start.3 = (f32[2,1,3,4,256]{4,3,2,1,0:T(4,128)S(1)}, f32[2,1,3,4,256]{4,3,2,1,0:T(4,128)S(1)}, u32[]{:S(2)}, u32[]{:S(2)}) collective-permute-start(f32[2,1,3,4,256]{4,3,2,1,0:T(4,128)S(1)} %get-tuple-element.15), channel_id=1, source_target_pairs={{4,0},{8,4},{12,8},{0,12},{5,1},{9,5},{13,9},{1,13},{6,2},{10,6},{... | collective-permute-start | bytes 73736 | tf_op jit(solution)/shard_map/ppermute | solution.py:23
  11.9 0.6 copy.25
  12.5 1.2 %collective-permute-done.2 = f32[2,1,3,4,256]{4,3,2,1,0:T(4,128)S(1)} collective-permute-done((f32[2,1,3,4,256]{4,3,2,1,0:T(4,128)S(1)}, f32[2,1,3,4,256]{4,3,2,1,0:T(4,128)S(1)}, u32[]{:S(2)}, u32[]{:S(2)}) %collective-permute-start.2) | collective-permute-done | bytes 24608 | tf_op jit(solution)/shard_map/ppermute | solution.py:20
  13.8 1.6 %collective-permute-start.4 = (f32[1,6,3,4,256]{4,3,2,1,0:T(4,128)S(1)}, f32[1,6,3,4,256]{4,3,2,1,0:T(4,128)S(1)}, u32[]{:S(2)}, u32[]{:S(2)}) collective-permute-start(f32[1,6,3,4,256]{4,3,2,1,0:T(4,128)S(1)} %get-tuple-element.12), channel_id=1, source_target_pairs={{0,16},{16,0},{1,17},{17,1},{2,18},{18,2},{3,19},{19,3},{4,20},{20... | collective-permute-start | bytes 221192 | tf_op jit(solution)/shard_map/ppermute | solution.py:20
  15.4 0.5 collective-permute-start.5
  15.9 2.3 %collective-permute-done.4 = f32[1,6,3,4,256]{4,3,2,1,0:T(4,128)S(1)} collective-permute-done((f32[1,6,3,4,256]{4,3,2,1,0:T(4,128)S(1)}, f32[1,6,3,4,256]{4,3,2,1,0:T(4,128)S(1)}, u32[]{:S(2)}, u32[]{:S(2)}) %collective-permute-start.4) | collective-permute-done | bytes 73760 | tf_op jit(solution)/shard_map/ppermute | solution.py:20
  18.3 1.5 %collective-permute-done.5 = f32[1,6,3,4,256]{4,3,2,1,0:T(4,128)S(1)} collective-permute-done((f32[1,6,3,4,256]{4,3,2,1,0:T(4,128)S(1)}, f32[1,6,3,4,256]{4,3,2,1,0:T(4,128)S(1)}, u32[]{:S(2)}, u32[]{:S(2)}) %collective-permute-start.5) | collective-permute-done | bytes 73760 | tf_op jit(solution)/shard_map/ppermute | solution.py:23
  20.0 0.4 select_reduce_fusion
  20.4 0.1 copy.24
  20.5 0.6 reshape.32.counts
  21.1 32.2 %forces.2 = (f32[8,3,256]{2,1,0:T(4,128)}, f32[8,3,256]{2,1,0:T(4,128)}) custom-call(s32[72]{0:T(128)} %reshape.32.counts, f32[4,6,3,4,256]{4,3,2,1,0:T(4,128)} %copy-done, f32[8,3,256]{2,1,0:T(4,128)} %bitcast.26), custom_call_target="tpu_custom_call" | custom-call | tf_op jit(solution)/shard_map/forces/pallas_call | solution.py:149
  53.3 0.5 collective-permute-start.6
  53.8 1.5 %collective-permute-done.7 = f32[2,4,1,3,256]{4,3,2,1,0:T(4,128)S(1)} collective-permute-done((f32[2,4,1,3,256]{4,3,2,1,0:T(4,128)}, f32[2,4,1,3,256]{4,3,2,1,0:T(4,128)S(1)}, u32[]{:S(2)}, u32[]{:S(2)}) %collective-permute-start.7) | collective-permute-done | bytes 24608 | tf_op jit(solution)/shard_map/ppermute | solution.py:23
  55.3 1.8 %collective-permute-done.6 = f32[2,4,1,3,256]{4,3,2,1,0:T(4,128)S(1)} collective-permute-done((f32[2,4,1,3,256]{4,3,2,1,0:T(4,128)}, f32[2,4,1,3,256]{4,3,2,1,0:T(4,128)S(1)}, u32[]{:S(2)}, u32[]{:S(2)}) %collective-permute-start.6) | collective-permute-done | bytes 24608 | tf_op jit(solution)/shard_map/ppermute | solution.py:20
  57.1 0.7 pad_maximum_fusion.7
  57.9 1.0 collective-permute-start.8
  58.9 2.9 %collective-permute-start.9 = (f32[2,1,3,3,256]{4,3,2,1,0:T(4,128)S(1)}, f32[2,1,3,3,256]{4,3,2,1,0:T(4,128)S(1)}, u32[]{:S(2)}, u32[]{:S(2)}) collective-permute-start(f32[2,1,3,3,256]{4,3,2,1,0:T(4,128)S(1)} %get-tuple-element.17), channel_id=1, source_target_pairs={{4,0},{8,4},{12,8},{0,12},{5,1},{9,5},{13,9},{1,13},{6,2},{10,6},{... | collective-permute-start | bytes 55304 | tf_op jit(solution)/shard_map/ppermute | solution.py:23
  61.7 1.8 %collective-permute-done.8 = f32[2,1,3,3,256]{4,3,2,1,0:T(4,128)S(1)} collective-permute-done((f32[2,1,3,3,256]{4,3,2,1,0:T(4,128)S(1)}, f32[2,1,3,3,256]{4,3,2,1,0:T(4,128)S(1)}, u32[]{:S(2)}, u32[]{:S(2)}) %collective-permute-start.8) | collective-permute-done | bytes 18464 | tf_op jit(solution)/shard_map/ppermute | solution.py:20
  63.6 1.4 %collective-permute-start.10 = (f32[1,6,3,3,256]{4,3,2,1,0:T(4,128)S(1)}, f32[1,6,3,3,256]{4,3,2,1,0:T(4,128)S(1)}, u32[]{:S(2)}, u32[]{:S(2)}) collective-permute-start(f32[1,6,3,3,256]{4,3,2,1,0:T(4,128)S(1)} %get-tuple-element.10), channel_id=1, source_target_pairs={{0,16},{16,0},{1,17},{17,1},{2,18},{18,2},{3,19},{19,3},{4,20},{20... | collective-permute-start | bytes 165896 | tf_op jit(solution)/shard_map/ppermute | solution.py:20
  65.0 0.7 collective-permute-start.11
  65.7 1.0 %slice.38 = f32[4,6,3,1,256]{4,3,2,1,0:T(1,128)S(1)} slice(f32[4,6,3,4,256]{4,3,2,1,0:T(4,128)} %copy-done), slice={[0:4], [0:6], [0:3], [3:4], [0:256]} | slice | bytes 147456 | tf_op jit(solution)/shard_map/slice | solution.py:177
  66.7 1.3 %collective-permute-done.10 = f32[1,6,3,3,256]{4,3,2,1,0:T(4,128)S(1)} collective-permute-done((f32[1,6,3,3,256]{4,3,2,1,0:T(4,128)S(1)}, f32[1,6,3,3,256]{4,3,2,1,0:T(4,128)S(1)}, u32[]{:S(2)}, u32[]{:S(2)}) %collective-permute-start.10) | collective-permute-done | bytes 55328 | tf_op jit(solution)/shard_map/ppermute | solution.py:20
  68.0 1.3 %collective-permute-done.11 = f32[1,6,3,3,256]{4,3,2,1,0:T(4,128)S(1)} collective-permute-done((f32[1,6,3,3,256]{4,3,2,1,0:T(4,128)S(1)}, f32[1,6,3,3,256]{4,3,2,1,0:T(4,128)S(1)}, u32[]{:S(2)}, u32[]{:S(2)}) %collective-permute-start.11) | collective-permute-done | bytes 55328 | tf_op jit(solution)/shard_map/ppermute | solution.py:23
  69.4 0.8 pad_maximum_fusion.1.src
  70.2 32.2 %forces.3 = (f32[8,3,256]{2,1,0:T(4,128)}, f32[8,3,256]{2,1,0:T(4,128)}) custom-call(s32[72]{0:T(128)} %reshape.32.counts, f32[4,6,3,4,256]{4,3,2,1,0:T(4,128)} %pad_maximum_fusion.1.src, f32[8,3,256]{2,1,0:T(4,128)} %get-tuple-element.7.vel), custom_call_target="tpu_custom_call" | custom-call | tf_op jit(solution)/shard_map/forces/pallas_call | solution.py:149
  102.4 1.4 %copy_bitcast_fusion.1 = (f32[3,2,4,1,256]{4,3,2,1,0:T(1,128)}, f32[3,2,4,1,256]{4,3,2,1,0:T(1,128)}) fusion(f32[2,4,1,3,256]{4,3,1,0,2:T(4,128)} %bitcast.28, f32[2,4,1,3,256]{4,3,1,0,2:T(4,128)} %bitcast.27), kind=kLoop, calls=%fused_computation.16 | loop fusion | bytes 98304 | tf_op jit(solution)/shard_map/transpose | solution.py:184
  (23 shorter events, 0.5 us)
Async XLA Ops:
  0.6 0.8 copy-start.3
  1.4 0.7 copy-start.4
  2.2 9.7 %copy-start.2 = (f32[3,2,4,1,256]{4,3,2,1,0:T(1,128)S(1)}, f32[3,2,4,1,256]{4,3,2,1,0:T(1,128)}, u32[]{:S(2)}) copy-start(f32[3,2,4,1,256]{4,3,2,1,0:T(1,128)} %param.5) | copy-start | bytes 73732
  2.2 4.2 %collective-permute-start.1 = (f32[2,4,1,4,256]{4,3,2,1,0:T(4,128)S(1)}, f32[2,4,1,4,256]{4,3,2,1,0:T(4,128)S(1)}, u32[]{:S(2)}, u32[]{:S(2)}) collective-permute-start(f32[2,4,1,4,256]{4,3,2,1,0:T(4,128)S(1)} %pad_maximum_fusion.4), channel_id=1, source_target_pairs={{1,0},{2,1},{3,2},{0,3},{5,4},{6,5},{7,6},{4,7},{9,8},{10,9},{11,1... | collective-permute-start | bytes 98312 | tf_op jit(solution)/shard_map/ppermute | solution.py:23
  4.7 3.3 %collective-permute-start = (f32[2,4,1,4,256]{4,3,2,1,0:T(4,128)S(1)}, f32[2,4,1,4,256]{4,3,2,1,0:T(4,128)S(1)}, u32[]{:S(2)}, u32[]{:S(2)}) collective-permute-start(f32[2,4,1,4,256]{4,3,2,1,0:T(4,128)S(1)} %pad_maximum_fusion.4), channel_id=1, source_target_pairs={{0,1},{1,2},{2,3},{3,0},{4,5},{5,6},{6,7},{7,4},{8,9},{9,10},{10,1... | collective-permute-start | bytes 98312 | tf_op jit(solution)/shard_map/ppermute | solution.py:20
  8.0 5.7 %collective-permute-start.2 = (f32[2,1,3,4,256]{4,3,2,1,0:T(4,128)S(1)}, f32[2,1,3,4,256]{4,3,2,1,0:T(4,128)S(1)}, u32[]{:S(2)}, u32[]{:S(2)}) collective-permute-start(f32[2,1,3,4,256]{4,3,2,1,0:T(4,128)S(1)} %get-tuple-element.14), channel_id=1, source_target_pairs={{0,4},{4,8},{8,12},{12,0},{1,5},{5,9},{9,13},{13,1},{2,6},{6,10},{... | collective-permute-start | bytes 73736 | tf_op jit(solution)/shard_map/ppermute | solution.py:20
  9.7 4.1 %collective-permute-start.3 = (f32[2,1,3,4,256]{4,3,2,1,0:T(4,128)S(1)}, f32[2,1,3,4,256]{4,3,2,1,0:T(4,128)S(1)}, u32[]{:S(2)}, u32[]{:S(2)}) collective-permute-start(f32[2,1,3,4,256]{4,3,2,1,0:T(4,128)S(1)} %get-tuple-element.15), channel_id=1, source_target_pairs={{4,0},{8,4},{12,8},{0,12},{5,1},{9,5},{13,9},{1,13},{6,2},{10,6},{... | collective-permute-start | bytes 73736 | tf_op jit(solution)/shard_map/ppermute | solution.py:23
  13.8 4.4 %collective-permute-start.4 = (f32[1,6,3,4,256]{4,3,2,1,0:T(4,128)S(1)}, f32[1,6,3,4,256]{4,3,2,1,0:T(4,128)S(1)}, u32[]{:S(2)}, u32[]{:S(2)}) collective-permute-start(f32[1,6,3,4,256]{4,3,2,1,0:T(4,128)S(1)} %get-tuple-element.12), channel_id=1, source_target_pairs={{0,16},{16,0},{1,17},{17,1},{2,18},{18,2},{3,19},{19,3},{4,20},{20... | collective-permute-start | bytes 221192 | tf_op jit(solution)/shard_map/ppermute | solution.py:20
  15.4 4.4 %collective-permute-start.5 = (f32[1,6,3,4,256]{4,3,2,1,0:T(4,128)S(1)}, f32[1,6,3,4,256]{4,3,2,1,0:T(4,128)S(1)}, u32[]{:S(2)}, u32[]{:S(2)}) collective-permute-start(f32[1,6,3,4,256]{4,3,2,1,0:T(4,128)S(1)} %get-tuple-element.13), channel_id=1, source_target_pairs={{16,0},{0,16},{17,1},{1,17},{18,2},{2,18},{19,3},{3,19},{20,4},{4,... | collective-permute-start | bytes 221192 | tf_op jit(solution)/shard_map/ppermute | solution.py:23
  19.8 1.3 %copy-start = (f32[4,6,3,4,256]{4,3,2,1,0:T(4,128)}, f32[4,6,3,4,256]{4,3,2,1,0:T(4,128)S(1)}, u32[]{:S(2)}) copy-start(f32[4,6,3,4,256]{4,3,2,1,0:T(4,128)S(1)} %pad_maximum_fusion.src) | copy-start | bytes 884740
  53.3 10.2 %copy-start.1 = (f32[8,3,256]{2,1,0:T(4,128)S(1)}, f32[8,3,256]{2,1,0:T(4,128)}, u32[]{:S(2)}) copy-start(f32[8,3,256]{2,1,0:T(4,128)} %get-tuple-element.6) | copy-start | bytes 73732
  53.3 2.0 %collective-permute-start.7 = (f32[2,4,1,3,256]{4,3,2,1,0:T(4,128)}, f32[2,4,1,3,256]{4,3,2,1,0:T(4,128)S(1)}, u32[]{:S(2)}, u32[]{:S(2)}) collective-permute-start(f32[2,4,1,3,256]{4,3,2,1,0:T(4,128)} %bitcast.21), channel_id=1, source_target_pairs={{1,0},{2,1},{3,2},{0,3},{5,4},{6,5},{7,6},{4,7},{9,8},{10,9},{11,1... | collective-permute-start | bytes 73736 | tf_op jit(solution)/shard_map/ppermute | solution.py:23
  53.3 3.8 %collective-permute-start.6 = (f32[2,4,1,3,256]{4,3,2,1,0:T(4,128)}, f32[2,4,1,3,256]{4,3,2,1,0:T(4,128)S(1)}, u32[]{:S(2)}, u32[]{:S(2)}) collective-permute-start(f32[2,4,1,3,256]{4,3,2,1,0:T(4,128)} %bitcast.22), channel_id=1, source_target_pairs={{0,1},{1,2},{2,3},{3,0},{4,5},{5,6},{6,7},{7,4},{8,9},{9,10},{10,1... | collective-permute-start | bytes 73736 | tf_op jit(solution)/shard_map/ppermute | solution.py:20
  57.9 5.7 %collective-permute-start.8 = (f32[2,1,3,3,256]{4,3,2,1,0:T(4,128)S(1)}, f32[2,1,3,3,256]{4,3,2,1,0:T(4,128)S(1)}, u32[]{:S(2)}, u32[]{:S(2)}) collective-permute-start(f32[2,1,3,3,256]{4,3,2,1,0:T(4,128)S(1)} %get-tuple-element.16), channel_id=1, source_target_pairs={{0,4},{4,8},{8,12},{12,0},{1,5},{5,9},{9,13},{13,1},{2,6},{6,10},{... | collective-permute-start | bytes 55304 | tf_op jit(solution)/shard_map/ppermute | solution.py:20
  58.9 4.7 %collective-permute-start.9 = (f32[2,1,3,3,256]{4,3,2,1,0:T(4,128)S(1)}, f32[2,1,3,3,256]{4,3,2,1,0:T(4,128)S(1)}, u32[]{:S(2)}, u32[]{:S(2)}) collective-permute-start(f32[2,1,3,3,256]{4,3,2,1,0:T(4,128)S(1)} %get-tuple-element.17), channel_id=1, source_target_pairs={{4,0},{8,4},{12,8},{0,12},{5,1},{9,5},{13,9},{1,13},{6,2},{10,6},{... | collective-permute-start | bytes 55304 | tf_op jit(solution)/shard_map/ppermute | solution.py:23
  63.6 4.4 %collective-permute-start.10 = (f32[1,6,3,3,256]{4,3,2,1,0:T(4,128)S(1)}, f32[1,6,3,3,256]{4,3,2,1,0:T(4,128)S(1)}, u32[]{:S(2)}, u32[]{:S(2)}) collective-permute-start(f32[1,6,3,3,256]{4,3,2,1,0:T(4,128)S(1)} %get-tuple-element.10), channel_id=1, source_target_pairs={{0,16},{16,0},{1,17},{17,1},{2,18},{18,2},{3,19},{19,3},{4,20},{20... | collective-permute-start | bytes 165896 | tf_op jit(solution)/shard_map/ppermute | solution.py:20
  65.0 4.4 %collective-permute-start.11 = (f32[1,6,3,3,256]{4,3,2,1,0:T(4,128)S(1)}, f32[1,6,3,3,256]{4,3,2,1,0:T(4,128)S(1)}, u32[]{:S(2)}, u32[]{:S(2)}) collective-permute-start(f32[1,6,3,3,256]{4,3,2,1,0:T(4,128)S(1)} %get-tuple-element.11), channel_id=1, source_target_pairs={{16,0},{0,16},{17,1},{1,17},{18,2},{2,18},{19,3},{3,19},{20,4},{4,... | collective-permute-start | bytes 165896 | tf_op jit(solution)/shard_map/ppermute | solution.py:23
